TPU v7x, 32 devices: a whole 2x2x4 slice. The times are simulated.
32 devices in a mesh: dp: 2 (over y), fsdp: 16 (over z, x, core).
Axes of the slice: x: 2, y: 2, z: 4, core: 2. Of those that a mesh axis runs over, the one named last changes fastest.
Arguments:
- tokens: bfloat16 [12288, 1024], P(('dp', 'fsdp')), may hold values from -6.5 to 6.5
- cotangent: bfloat16 [12288, 1024], P(('dp', 'fsdp')), may hold values from -6 to 6
- patch_count: int32 [32], P(('dp', 'fsdp')), may hold values from 96 to 384, as said below
- image_starts: int32 [32, 8], P(('dp', 'fsdp')), may hold values from 0 to 384, as said below
- qkv_weight: bfloat16 [1024, 3072], P('fsdp'), may hold values from -8 to 8
- proj_weight: bfloat16 [1024, 1024], P('fsdp'), may hold values from -0.1875 to 0.1875
- norm_gain: bfloat16 [1024], P('fsdp'), may hold values from 0.25 to 1.75
- norm_shift: bfloat16 [1024], P('fsdp'), may hold values from -3 to 3
Outputs:
- grad_tokens: bfloat16 [12288, 1024], P(('dp', 'fsdp'))
- qkv_grad: float32 [1024, 3072], P('fsdp')
- proj_grad: float32 [1024, 1024], P('fsdp')
- gain_grad: float32 [1024], P('fsdp')
- shift_grad: float32 [1024], P('fsdp')
Inputs may be any that keep to these rules, and one draw needn't show every extreme that they name: `patch_count`: at least one device has all 384 slots live; live slots of a device come first. `image_starts`: per device, non-decreasing and first 0; an image runs from its start to the next start or to the device's patch count; a start equal to the patch count marks an absent image; no image has more than 192 patches.
All inputs are finite; a program needn't handle non-finite values.
Results may differ from a plain program's by a relative error of at most 0.025.
The roundings to bfloat16 on the way count: a program that leaves them out, or rounds other values in their place, can miss the bound.
Values may be sent and summed in bfloat16 or wider, within the bound.
A program may use at most 128 MiB of HBM per device.

v0:
```python
import math

import jax
import jax.numpy as jnp
from jax import lax
from jax.sharding import PartitionSpec as P

D = 1024
HEAD_DIM = 64
HEADS = 16


norm_eps = 1e-06
masked_score = -1e30


def block_backward(
    block_tokens, block_cot, live_count, starts, qkv_weight, proj_weight, norm_gain, norm_shift
):
    rows = block_tokens.shape[0]
    factor = HEAD_DIM ** (-0.5)
    position = jnp.arange(rows, dtype=jnp.int32)
    live = position < live_count
    segment = jnp.sum((starts[None, :] <= position[:, None]).astype(jnp.int32), axis=1)
    allowed = live[:, None] & live[None, :] & (segment[:, None] == segment[None, :])
    source = block_tokens.astype(jnp.float32)
    center = jnp.mean(source, axis=1, keepdims=True)
    centered = source - center
    variance = jnp.mean(centered * centered, axis=1, keepdims=True)
    inverse = lax.rsqrt(variance + norm_eps)
    normed = centered * inverse
    gain = norm_gain.astype(jnp.float32)
    hidden = (normed * gain + norm_shift.astype(jnp.float32)).astype(jnp.bfloat16)
    qkv = jnp.dot(hidden, qkv_weight, preferred_element_type=jnp.float32).astype(jnp.bfloat16)
    split = qkv.reshape(rows, 3, HEADS, HEAD_DIM)
    queries = split[:, 0]
    keys = split[:, 1]
    values = split[:, 2]
    scores = jnp.einsum("qhe,khe->hqk", queries, keys, preferred_element_type=jnp.float32) * factor
    scores = jnp.where(allowed[None], scores, masked_score)
    row_max = jnp.max(scores, axis=2, keepdims=True)
    expon = jnp.exp(scores - row_max)
    probs = expon / jnp.sum(expon, axis=2, keepdims=True)
    probs_low = probs.astype(jnp.bfloat16)
    attended = (
        jnp.einsum("hqk,khe->qhe", probs_low, values, preferred_element_type=jnp.float32)
        .reshape(rows, D)
        .astype(jnp.bfloat16)
    )
    masked_cot = jnp.where(live[:, None], block_cot, jnp.zeros_like(block_cot))
    proj_term = jnp.dot(attended.T, masked_cot, preferred_element_type=jnp.float32)
    grad_attended = jnp.dot(masked_cot, proj_weight.T, preferred_element_type=jnp.float32).astype(
        jnp.bfloat16
    )
    grad_heads = grad_attended.reshape(rows, HEADS, HEAD_DIM)
    grad_probs = jnp.einsum("qhe,khe->hqk", grad_heads, values, preferred_element_type=jnp.float32)
    grad_values = jnp.einsum(
        "hqk,qhe->khe", probs_low, grad_heads, preferred_element_type=jnp.float32
    ).astype(jnp.bfloat16)
    grad_scores = probs * (grad_probs - jnp.sum(probs * grad_probs, axis=2, keepdims=True)) * factor
    grad_scores = grad_scores.astype(jnp.bfloat16)
    grad_queries = jnp.einsum(
        "hqk,khe->qhe", grad_scores, keys, preferred_element_type=jnp.float32
    ).astype(jnp.bfloat16)
    grad_keys = jnp.einsum(
        "hqk,qhe->khe", grad_scores, queries, preferred_element_type=jnp.float32
    ).astype(jnp.bfloat16)
    grad_qkv = jnp.stack([grad_queries, grad_keys, grad_values], axis=1).reshape(rows, 3 * D)
    qkv_term = jnp.dot(hidden.T, grad_qkv, preferred_element_type=jnp.float32)
    grad_hidden = jnp.dot(grad_qkv, qkv_weight.T, preferred_element_type=jnp.float32)
    gain_term = jnp.sum(grad_hidden * normed, axis=0)
    shift_term = jnp.sum(grad_hidden, axis=0)
    grad_normed = grad_hidden * gain
    inner = grad_normed - jnp.mean(grad_normed, axis=1, keepdims=True)
    inner = inner - normed * jnp.mean(grad_normed * normed, axis=1, keepdims=True)
    grad_block = (block_cot.astype(jnp.float32) + inverse * inner).astype(jnp.bfloat16)
    return (grad_block, qkv_term, proj_term, gain_term, shift_term)


def per_device(
    tokens, cotangent, patch_count, image_starts, qkv_weight, proj_weight, norm_gain, norm_shift
):
    whole_qkv, whole_proj, whole_gain, whole_shift = (
        lax.all_gather(qkv_weight, "fsdp", axis=0, tiled=True),
        lax.all_gather(proj_weight, "fsdp", axis=0, tiled=True),
        lax.all_gather(norm_gain, "fsdp", axis=0, tiled=True),
        lax.all_gather(norm_shift, "fsdp", axis=0, tiled=True),
    )
    grad_block, qkv_term, proj_term, gain_term, shift_term = block_backward(
        tokens,
        cotangent,
        patch_count[0],
        image_starts[0],
        whole_qkv,
        whole_proj,
        whole_gain,
        whole_shift,
    )
    replicas = lax.axis_size("dp")
    owners = lax.axis_size("fsdp")
    factor = 1.0 / math.sqrt(tokens.shape[0] * replicas * owners)
    terms = (qkv_term, proj_term, gain_term, shift_term)
    summed = (
        lax.psum_scatter(
            terms[0].astype(jnp.bfloat16), "fsdp", scatter_dimension=0, tiled=True
        ).astype(jnp.float32),
        lax.psum_scatter(
            terms[1].astype(jnp.bfloat16), "fsdp", scatter_dimension=0, tiled=True
        ).astype(jnp.float32),
        lax.psum_scatter(
            terms[2].astype(jnp.bfloat16), "fsdp", scatter_dimension=0, tiled=True
        ).astype(jnp.float32),
        lax.psum_scatter(
            terms[3].astype(jnp.bfloat16), "fsdp", scatter_dimension=0, tiled=True
        ).astype(jnp.float32),
    )
    summed = (
        lax.psum(summed[0].astype(jnp.bfloat16), "dp").astype(jnp.float32),
        lax.psum(summed[1].astype(jnp.bfloat16), "dp").astype(jnp.float32),
        lax.psum(summed[2].astype(jnp.bfloat16), "dp").astype(jnp.float32),
        lax.psum(summed[3].astype(jnp.bfloat16), "dp").astype(jnp.float32),
    )
    return (
        grad_block,
        summed[0] * factor,
        summed[1] * factor,
        summed[2] * factor,
        summed[3] * factor,
    )


def solution(mesh):
    placed = (
        P(("dp", "fsdp"), None),
        P(("dp", "fsdp"), None),
        P(("dp", "fsdp")),
        P(("dp", "fsdp"), None),
        P("fsdp", None),
        P("fsdp", None),
        P("fsdp"),
        P("fsdp"),
    )
    return jax.shard_map(
        per_device,
        mesh=mesh,
        in_specs=placed,
        out_specs=(P(("dp", "fsdp"), None), P("fsdp", None), P("fsdp", None), P("fsdp"), P("fsdp")),
        check_vma=False,
    )
```

profile of v0, /device:TPU:0, one launch (start us, length us, event | category | flops | bytes accessed | tf_op | source)
XLA Modules:
  0.0 308.9 jit_solution(15544048254684198745)
XLA Ops:
  7.2 0.0 all-gather.3.cloned.1.call-start
  7.2 0.7 all-gather.3.cloned.1.call-update
  7.9 0.0 all-gather.5.cloned.1.call-start
  7.9 0.7 all-gather.5.cloned.1.call-update
  8.6 0.0 reduce-scatter.5.cloned.1.call-start
  9.4 1.3 fusion.69
  11.3 0.8 dynamic-update-slice
  12.2 0.8 dynamic-update-slice.1
  13.0 35.6 %all-reduce.5 = (bf16[1024]{0:T(1024)(128)(2,1)S(1)}, bf16[1024]{0:T(1024)(128)(2,1)S(1)}) all-reduce(bf16[1024]{0:T(1024)(128)(2,1)S(1)} %dynamic-update-slice.1, bf16[1024]{0:T(1024)(128)(2,1)S(1)} %dynamic-update-slice), channel_id=1, replica_groups=mesh['dp'=2,'fsdp'=16] {'fsdp'}, use_global_device_ids=true, to_apply=%add.1 | all-reduce | flops 2048 | bytes 8192
  48.6 0.7 convert_reduce_fusion.1
  49.3 1.3 convert_reduce_fusion
  50.7 1.5 fusion.33
  52.2 0.2 compare_and_fusion
  52.4 22.1 %all-gather.3.cloned.1.call-done = bf16[1024,3072]{1,0:T(8,128)(2,1)} async-done(((bf16[64,3072]{1,0:T(8,128)(2,1)}), bf16[1024,3072]{1,0:T(8,128)(2,1)}) %all-gather.3.cloned.1.call-update) | async-done | bytes 6291472 | tf_op jit(solution)/shard_map/all_gather | solution.py:84
  74.4 7.2 %convolution_convert_fusion.1 = bf16[384,3072]{1,0:T(8,128)(2,1)} fusion(bf16[1024,3072]{1,0:T(8,128)(2,1)} %all-gather.3.cloned.1.call-done, bf16[384,1024]{1,0:T(8,128)(2,1)} %param.8, f32[1024]{0:T(1024)S(1)} %convert_element_type.95, f32[1024]{0:T(1024)S(1)} %convert_element_type.94, f32[384]{0:T(512)S(1)} %add_rsqrt_fusion, ...), kind=kOutput, calls=%fused_computation.15 | convolution fusion | flops 2419458048 | bytes 9448448 | tf_op jit(solution)/shard_map/dot_general | solution.py:34
  81.6 3.0 copy.34
  84.7 5.6 %fusion.70 = (f32[16,384]{1,0:T(8,128)S(1)}, f32[16,384,384]{1,2,0:T(8,128)}) fusion(pred[384,384]{0,1:T(8,128)(4,1)S(1)} %compare_and_fusion, bf16[384,3,16,64]{0,3,2,1:T(8,128)(2,1)S(1)} %bitcast.59), kind=kOutput, calls=%fused_computation.76 | convolution fusion | flops 311427456 | bytes 11182080 | tf_op jit(solution)/shard_map/sub | solution.py:42
  90.3 0.0 copy-start.3
  90.3 4.7 %fusion.37 = bf16[16,64,384]{2,1,0:T(8,128)(2,1)S(1)} fusion(bf16[384,3,16,64]{0,3,2,1:T(8,128)(2,1)S(1)} %bitcast.60, f32[16,384,384]{1,2,0:T(8,128)} %get-tuple-element.20, f32[16,384]{1,0:T(8,128)S(1)} %get-tuple-element.19), kind=kOutput, calls=%fused_computation.40 | convolution fusion | flops 307101696 | bytes 11034624 | tf_op jit(solution)/shard_map/hqk,khe->qhe/dot_general | solution.py:46
  94.9 0.0 copy-done.3
  94.9 2.7 convolution_convert_fusion.2
  97.6 0.0 reduce-scatter.5.cloned.1.call-update
  97.7 0.2 reduce-scatter.3.cloned.1.call-start
  97.9 18.8 %all-gather.5.cloned.1.call-done = bf16[1024,1024]{1,0:T(8,128)(2,1)} async-done(((bf16[64,1024]{1,0:T(8,128)(2,1)}), bf16[1024,1024]{1,0:T(8,128)(2,1)}) %all-gather.5.cloned.1.call-update) | async-done | bytes 2097168 | tf_op jit(solution)/shard_map/all_gather | solution.py:85
  116.7 3.5 %convolution_convert_fusion.3 = bf16[384,1024]{1,0:T(8,128)(2,1)} fusion(bf16[1024,1024]{1,0:T(8,128)(2,1)} %all-gather.5.cloned.1.call-done, bf16[384,1024]{1,0:T(8,128)(2,1)S(1)} %copy-done.3, pred[384]{0:T(512)(128)(4,1)S(1)} %iota_compare_fusion.1), kind=kOutput, calls=%fused_computation.43 | convolution fusion | flops 806092800 | bytes 3670400 | tf_op jit(solution)/shard_map/dot_general | solution.py:52
  120.2 1.5 copy.35
  121.7 5.1 %fusion.57 = f32[16,384,384]{1,2,0:T(8,128)} fusion(bf16[384,16,64]{0,2,1:T(8,128)(2,1)S(1)} %bitcast.64, bf16[384,3,16,64]{0,3,2,1:T(8,128)(2,1)S(1)} %bitcast.61), kind=kOutput, calls=%fused_computation.54 | convolution fusion | flops 301989888 | bytes 11010048 | tf_op jit(solution)/shard_map/qhe,khe->hqk/dot_general | solution.py:56
  126.8 15.5 %fusion.49 = bf16[384,1,16,64]{0,3,2,1:T(8,128)(2,1)} fusion(f32[16,384,384]{1,2,0:T(8,128)} %fusion.57, bf16[384,3,16,64]{0,3,2,1:T(8,128)(2,1)S(1)} %bitcast.62, f32[16,384,384]{1,2,0:T(8,128)} %get-tuple-element.20, f32[16,384]{1,0:T(8,128)S(1)} %get-tuple-element.19), kind=kOutput, calls=%fused_computation.46 | convolution fusion | flops 318904704 | bytes 39370752 | tf_op jit(solution)/shard_map/hqk,khe->qhe/dot_general | solution.py:62
  142.4 14.7 %fusion.46 = bf16[384,1,16,64]{0,3,2,1:T(8,128)(2,1)} fusion(f32[16,384,384]{1,2,0:T(8,128)} %fusion.57, bf16[384,3,16,64]{0,3,2,1:T(8,128)(2,1)S(1)} %bitcast.63, f32[16,384,384]{1,2,0:T(8,128)} %get-tuple-element.20, f32[16,384]{1,0:T(8,128)S(1)} %get-tuple-element.19), kind=kOutput, calls=%fused_computation.45 | convolution fusion | flops 318904704 | bytes 39370752 | tf_op jit(solution)/shard_map/hqk,qhe->khe/dot_general | solution.py:65
  157.1 0.0 copy-start.1
  157.1 0.0 copy-start.2
  157.1 5.7 %fusion.52 = bf16[384,1,16,64]{0,3,2,1:T(8,128)(2,1)S(1)} fusion(bf16[384,16,64]{0,2,1:T(8,128)(2,1)S(1)} %bitcast.65, f32[16,384,384]{1,2,0:T(8,128)} %get-tuple-element.20, f32[16,384]{1,0:T(8,128)S(1)} %get-tuple-element.19), kind=kOutput, calls=%fused_computation.47 | convolution fusion | flops 307101696 | bytes 11034624 | tf_op jit(solution)/shard_map/hqk,qhe->khe/dot_general | solution.py:57
  162.8 0.0 copy-done.1
  162.8 0.0 copy-done.2
  162.8 0.0 copy-start
  162.8 0.3 pad_maximum_fusion
  163.1 0.8 copy-done
  163.9 5.8 %convolution_convert_fusion = bf16[1024,3072]{1,0:T(8,128)(2,1)} fusion(bf16[384,3072]{0,1:T(8,128)(2,1)S(1)} %bitcast.66, bf16[384,1024]{1,0:T(8,128)(2,1)S(1)} %copy-done, f32[1024]{0:T(1024)S(1)} %convert_element_type.95, f32[1024]{0:T(1024)S(1)} %convert_element_type.94, f32[384]{0:T(512)S(1)} %add_rsqrt_fusion, f32[384]{0:T(512)S(1)} %broadcast_multiply_fusion.2), kind=kOutput, calls=%fused_computation.8 | convolution fusion | flops 2421424128 | bytes 9448448 | tf_op jit(solution)/shard_map/dot_general | solution.py:69
  169.8 0.0 reduce-scatter.3.cloned.1.call-update
  169.8 0.0 all-reduce.10.cloned.1.call-start
  170.5 6.9 %fusion.32 = (bf16[1024]{0:T(1024)(128)(2,1)S(1)}, f32[384]{0:T(512)S(1)}, f32[384]{0:T(512)S(1)}, bf16[1024]{0:T(1024)(128)(2,1)S(1)}, f32[384,1024]{1,0:T(8,128)}) fusion(bf16[384,1024]{1,0:T(8,128)(2,1)S(1)} %copy-done, f32[384]{0:T(512)S(1)} %add_rsqrt_fusion, f32[384]{0:T(512)S(1)} %broadcast_multiply_fusion.2, f32[1024]{0:T(1024)S(1)} %convert_element_type.94, ...), kind=kOutput, calls=%fused_computation.37 | convolution fusion | flops 2419848192 | bytes 11024384 | tf_op jit(solution)/shard_map/dot_general | solution.py:70
  177.4 31.3 %all-reduce.4 = (bf16[1024]{0:T(1024)(128)(2,1)S(1)}, bf16[1024]{0:T(1024)(128)(2,1)S(1)}) all-reduce(bf16[1024]{0:T(1024)(128)(2,1)S(1)} %get-tuple-element.5, bf16[1024]{0:T(1024)(128)(2,1)S(1)} %get-tuple-element.8), channel_id=4, replica_groups=mesh['dp'=2,'fsdp'=16] {'fsdp'}, use_global_device_ids=true, to_apply=%region_13.14.clone | all-reduce | flops 2048 | bytes 8192
  208.7 0.1 dynamic-slice.5
  208.8 0.1 dynamic-slice.3
  208.9 4.9 %all-reduce.6 = (bf16[64]{0:T(256)(128)(2,1)S(1)}, bf16[64]{0:T(256)(128)(2,1)S(1)}) all-reduce(bf16[64]{0:T(256)(128)(2,1)S(1)} %dynamic-slice.3, bf16[64]{0:T(256)(128)(2,1)S(1)} %dynamic-slice.5), channel_id=1, replica_groups=mesh['dp'=2,'fsdp'=16] {'dp'}, use_global_device_ids=true, to_apply=%region_14.15 | all-reduce | flops 128 | bytes 512 | tf_op jit(solution)/shard_map/psum | solution.py:120
  213.8 0.0 reduce-scatter.5.cloned.1.call-done
  213.8 55.1 %reduce-scatter.3.cloned.1.call-done = bf16[64,3072]{1,0:T(8,128)(2,1)} async-done(((bf16[1024,3072]{1,0:T(8,128)(2,1)}), bf16[64,3072]{1,0:T(8,128)(2,1)}) %reduce-scatter.3.cloned.1.call-update) | async-done | bytes 393232 | tf_op jit(solution)/shard_map/reduce_scatter | solution.py:104
  268.9 0.0 all-reduce.10.cloned.1.call-update
  268.9 0.5 convert_multiply_fusion.2
  269.4 3.2 %fusion.31 = bf16[384,1024]{1,0:T(8,128)(2,1)} fusion(bf16[384,1024]{1,0:T(8,128)(2,1)S(1)} %copy-done, bf16[384,1024]{1,0:T(8,128)(2,1)} %param.9, f32[384,1024]{1,0:T(8,128)} %get-tuple-element.21, f32[384]{0:T(512)S(1)} %get-tuple-element.22, f32[384]{0:T(512)S(1)} %get-tuple-element.23, f32[1024]{0:T(1024)S(1)} %convert_element_type.94, ...), kind=kLoop, calls=%fused_computation.36 | loop fusion | flops 4325376 | bytes 3942400 | tf_op jit(solution)/shard_map/convert_element_type | solution.py:76
  272.6 26.2 %all-reduce.10.cloned.1.call-done = (bf16[64,3072]{1,0:T(8,128)(2,1)}, bf16[64,1024]{1,0:T(8,128)(2,1)}) async-done(((bf16[64,3072]{1,0:T(8,128)(2,1)}, bf16[64,1024]{1,0:T(8,128)(2,1)}), (bf16[64,3072]{1,0:T(8,128)(2,1)}, bf16[64,1024]{1,0:T(8,128)(2,1)})) %all-reduce.10.cloned.1.call-update) | async-done | bytes 524304 | tf_op jit(solution)/shard_map/psum | solution.py:118
  298.8 1.9 convert_multiply_fusion
  300.7 1.6 convert_multiply_fusion.1
  (8 shorter events, 0.0 us)
Async XLA Ops:
  7.2 67.3 %all-gather.3.cloned.1.call-start = ((), (), s32[]{:S(2)}) async-start(), calls=%async_computation.2 | async-start | bytes 6684672 | tf_op jit(solution)/shard_map/all_gather | solution.py:84
  7.9 108.8 %all-gather.5.cloned.1.call-start = ((), (), s32[]{:S(2)}) async-start(), calls=%async_computation.3 | async-start | bytes 2228224 | tf_op jit(solution)/shard_map/all_gather | solution.py:85
  8.6 205.2 %reduce-scatter.5.cloned.1.call-start = ((), (), s32[]{:S(2)}) async-start(), calls=%async_computation.5 | async-start | bytes 2228224 | tf_op jit(solution)/shard_map/reduce_scatter | solution.py:107
  90.3 4.7 %copy-start.3 = (bf16[384,1024]{1,0:T(8,128)(2,1)S(1)}, bf16[384,1024]{1,0:T(8,128)(2,1)}, u32[]{:S(2)}) copy-start(bf16[384,1024]{1,0:T(8,128)(2,1)} %param.9) | copy-start | bytes 2359300
  97.7 171.2 %reduce-scatter.3.cloned.1.call-start = ((), (), s32[]{:S(2)}) async-start(), calls=%async_computation.4 | async-start | bytes 6684672 | tf_op jit(solution)/shard_map/reduce_scatter | solution.py:104
  157.1 5.7 %copy-start.1 = (bf16[384,1,16,64]{0,3,2,1:T(8,128)(2,1)S(1)}, bf16[384,1,16,64]{0,3,2,1:T(8,128)(2,1)}, u32[]{:S(2)}) copy-start(bf16[384,1,16,64]{0,3,2,1:T(8,128)(2,1)} %fusion.49) | copy-start | bytes 2359300
  157.1 5.7 %copy-start.2 = (bf16[384,1,16,64]{0,3,2,1:T(8,128)(2,1)S(1)}, bf16[384,1,16,64]{0,3,2,1:T(8,128)(2,1)}, u32[]{:S(2)}) copy-start(bf16[384,1,16,64]{0,3,2,1:T(8,128)(2,1)} %fusion.46) | copy-start | bytes 2359300
  162.8 1.1 copy-start
  169.8 129.0 %all-reduce.10.cloned.1.call-start = ((), (), s32[]{:S(2)}) async-start(), calls=%async_computation.6 | async-start | bytes 1048576 | tf_op jit(solution)/shard_map/psum | solution.py:118
Sparse Core Ops, SparseCore 0:
  10.3 64.1 all-gather.2
  76.6 40.0 all-gather.4
  120.5 60.5 reduce-scatter.4
  184.8 83.9 reduce-scatter.2
  271.0 27.7 all-reduce.9
where the time goes:
time: 310 us; the launch traced here: 309 us
  waiting for transfers between devices  124 us (40%)
  matrix products  77.4 us (25%)
  blocking collectives  71.8 us (23%)
  between operations  15.8 us (5%)
  other arithmetic  11.3 us (4%)
  local copies, waits for them, and re-layouts  8.52 us (3%)
    unnamed x2, blocking collectives  66.9 us
    reduce_scatter x1, waiting for transfers between devices, per_device(): lax.psum_scatter(terms[0].astype(jnp.bfloat16), 'fsdp', scatter_dimension...  55.1 us
    psum x1, waiting for transfers between devices, per_device(): lax.psum(summed[0].astype(jnp.bfloat16), 'dp').astype(jnp.float32)  26.2 us
    all_gather x1, waiting for transfers between devices, per_device(): lax.all_gather(qkv_weight, 'fsdp', axis=0, tiled=True)  22.1 us
    all_gather x1, waiting for transfers between devices, per_device(): lax.all_gather(proj_weight, 'fsdp', axis=0, tiled=True)  18.8 us
    dot_general x1, matrix products, block_backward(): jnp.einsum('hqk,khe->qhe', grad_scores, keys, preferred_element_type=jnp....  15.5 us
    dot_general x1, matrix products, block_backward(): jnp.einsum('hqk,qhe->khe', grad_scores, queries, preferred_element_type=j...  14.7 us
    dot_general x1, matrix products, block_backward(): jnp.dot(hidden, qkv_weight, preferred_element_type=jnp.float32)  7.19 us
  transfers between devices with their start and end apart: 5, of which 4 were waited for; matrix products, arithmetic and copies ran while one was open for 30% of the time, Pallas kernels for 0%

commit v1 on v0

--- a/solution.py
+++ b/solution.py
@@ -1,8 +1,11 @@
+import functools
 import math
 
 import jax
 import jax.numpy as jnp
 from jax import lax
+from jax.experimental import pallas as pl
+from jax.experimental.pallas import tpu as pltpu
 from jax.sharding import PartitionSpec as P
 
 D = 1024
@@ -77,15 +80,404 @@
     return (grad_block, qkv_term, proj_term, gain_term, shift_term)
 
 
+LANES = 128
+CORES = 2
+LONG = 4
+
+
+def grid_of(owners):
+    long_size = LONG if owners % (LONG * CORES) == 0 else 1
+    return long_size, owners // (long_size * CORES)
+
+
+def inside(at, size):
+    return jnp.logical_and(at >= 0, at < size)
+
+
+def place(owners):
+    long_size, across_size = grid_of(owners)
+    me = lax.axis_index("fsdp")
+    core = lax.rem(me, CORES)
+    across = lax.rem(lax.div(me, CORES), across_size)
+    along = lax.div(me, CORES * across_size)
+    return me, along, across, core
+
+
+def neighbours(owners):
+    long_size, across_size = grid_of(owners)
+    me, along, across, core = place(owners)
+    return (
+        (along + 1 < long_size, me + CORES * across_size),
+        (along >= 1, me - CORES * across_size),
+        (across + 1 < across_size, me + CORES),
+        (across >= 1, me - CORES),
+        (core >= 0, me + 1 - 2 * core),
+    )
+
+
+def greet(owners, replicas):
+    barrier = pltpu.get_barrier_semaphore()
+    count = jnp.int32(0)
+    for there, target in neighbours(owners):
+        count = count + there.astype(jnp.int32)
+
+        @pl.when(there)
+        def _():
+            pl.semaphore_signal(barrier, inc=1, device_id={"fsdp": target})
+
+    mine = lax.axis_index("dp")
+    for step in range(1, replicas):
+        pl.semaphore_signal(
+            barrier, inc=1, device_id={"dp": lax.rem(mine + step, replicas)}
+        )
+    pl.semaphore_wait(barrier, count + (replicas - 1))
+
+
+def gather_kernel(owners, own_ref, qkv_ref, proj_ref, small_ref, held, send_sem, recv_sem):
+    long_size, across_size = grid_of(owners)
+    me, along, across, core = place(owners)
+    rows = own_ref.shape[0]
+    width = qkv_ref.shape[1]
+    square = proj_ref.shape[1]
+    greet(owners, 1)
+    steps = [(0, 0)]
+    for total in range(1, long_size + across_size - 1):
+        for far in range(min(total, long_size - 1), -1, -1):
+            side = total - far
+            if side >= across_size:
+                continue
+            for up in (1, -1) if far else (1,):
+                for out in (1, -1) if side else (1,):
+                    steps.append((up * far, out * side))
+
+    def copies(up, out):
+        at_long, at_across = along + up, across + out
+        piece = (at_long * across_size + at_across) * CORES + core
+        source = own_ref if up == 0 and out == 0 else held.at[piece]
+        there = neighbours(owners)
+        use = [out == 0 and up <= 0, out == 0 and up >= 0, out <= 0, out >= 0, True]
+        made = []
+        for way in range(5):
+            if use[way]:
+                copy = pltpu.make_async_remote_copy(
+                    src_ref=source,
+                    dst_ref=held.at[piece],
+                    send_sem=send_sem.at[way, piece],
+                    recv_sem=recv_sem.at[piece],
+                    device_id={"fsdp": there[way][1]},
+                )
+                made.append((there[way][0], copy))
+        there_is = jnp.logical_and(inside(at_long, long_size), inside(at_across, across_size))
+        return piece, there_is, made
+
+    def arrived(piece):
+        pltpu.make_async_remote_copy(
+            src_ref=own_ref,
+            dst_ref=held.at[piece],
+            send_sem=send_sem.at[0, piece],
+            recv_sem=recv_sem.at[piece],
+            device_id={"fsdp": me + 1 - 2 * core},
+        ).wait_recv()
+
+    for up, out in steps:
+        piece, there_is, made = copies(up, out)
+
+        @pl.when(there_is)
+        def _():
+            if up != 0 or out != 0:
+                arrived(piece)
+            for exists, copy in made:
+                @pl.when(exists)
+                def _():
+                    copy.start()
+
+    qkv_ref[pl.ds(pl.multiple_of(me * rows, rows), rows), :] = own_ref[:, :width]
+    proj_ref[pl.ds(pl.multiple_of(me * rows, rows), rows), :] = own_ref[:, width : width + square]
+    small_ref[me] = own_ref[:, width + square :]
+
+    def unpack(pair, carry):
+        piece = pair * CORES + 1 - core
+        arrived(piece)
+        for one in range(CORES):
+            at = pair * CORES + one
+
+            @pl.when(at != me)
+            def _():
+                start = pl.ds(pl.multiple_of(at * rows, rows), rows)
+                qkv_ref[start, :] = held[at, :, :width]
+                proj_ref[start, :] = held[at, :, width : width + square]
+                small_ref[at] = held[at, :, width + square :]
+
+        return carry
+
+    lax.fori_loop(0, owners // CORES, unpack, 0)
+    for up, out in steps:
+        piece, there_is, made = copies(up, out)
+
+        @pl.when(there_is)
+        def _():
+            for exists, copy in made:
+                @pl.when(exists)
+                def _():
+                    copy.wait_send()
+
+
+def gather_all(owners, own, width, square):
+    rows, packed = own.shape
+    return pl.pallas_call(
+        functools.partial(gather_kernel, owners),
+        name="gather_all",
+        out_shape=(
+            jax.ShapeDtypeStruct((owners * rows, width), jnp.bfloat16),
+            jax.ShapeDtypeStruct((owners * rows, square), jnp.bfloat16),
+            jax.ShapeDtypeStruct((owners, rows, LANES), jnp.bfloat16),
+        ),
+        in_specs=[pl.BlockSpec(memory_space=pltpu.VMEM)],
+        out_specs=(pl.BlockSpec(memory_space=pltpu.VMEM),) * 3,
+        scratch_shapes=[
+            pltpu.VMEM((owners, rows, packed), jnp.bfloat16),
+            pltpu.SemaphoreType.DMA((5, owners)),
+            pltpu.SemaphoreType.DMA((owners,)),
+        ],
+        compiler_params=pltpu.CompilerParams(
+            collective_id=0, has_side_effects=True, vmem_limit_bytes=48 * 2**20
+        ),
+    )(own)
+
+
+def scatter_kernel(
+    owners, replicas, factor,
+    qkv_ref, proj_ref, small_ref, qkv_out, proj_out, small_out,
+    from_qkv, from_proj, from_small, part, from_left, from_right, line, from_low, from_high,
+    mine_ref, twins, core_send, core_recv, across_send, across_recv, long_send, long_recv,
+    twin_send, twin_recv,
+):
+    long_size, across_size = grid_of(owners)
+    me, along, across, core = place(owners)
+    rows = qkv_out.shape[0]
+    width = qkv_out.shape[1]
+    square = proj_out.shape[1]
+    pairs = owners // CORES
+    wide = jnp.float32
+    low = jnp.bfloat16
+    greet(owners, replicas)
+    sibling = {"fsdp": me + 1 - 2 * core}
+
+    order = [
+        (step_long, step_across)
+        for step_long in range(long_size)
+        for step_across in range(across_size)
+    ]
+
+    def spot(step_long, step_across):
+        at_long = lax.rem(along + 1 + step_long, long_size)
+        at_across = lax.rem(across + 1 + step_across, across_size)
+        return at_long, at_across
+
+    def core_copies(at_long, at_across):
+        pair = at_long * across_size + at_across
+        block = pair * CORES + 1 - core
+        start = pl.ds(pl.multiple_of(block * rows, rows), rows)
+        made = []
+        for kind, (src, dst) in enumerate(
+            (
+                (qkv_ref.at[start, :], from_qkv.at[pair]),
+                (proj_ref.at[start, :], from_proj.at[pair]),
+                (small_ref.at[block], from_small.at[pair]),
+            )
+        ):
+            made.append(
+                pltpu.make_async_remote_copy(
+                    src_ref=src,
+                    dst_ref=dst,
+                    send_sem=core_send.at[kind, pair],
+                    recv_sem=core_recv.at[kind, pair],
+                    device_id=sibling,
+                )
+            )
+        return made
+
+    for steps in order:
+        for copy in core_copies(*spot(*steps)):
+            copy.start()
+
+    def across_copy(at_long, at_across, way):
+        pair = at_long * across_size + at_across
+        landing = from_left if way > 0 else from_right
+        side = 0 if way > 0 else 1
+        return pltpu.make_async_remote_copy(
+            src_ref=part.at[pair],
+            dst_ref=landing.at[pair],
+            send_sem=across_send.at[side, pair],
+            recv_sem=across_recv.at[side, pair],
+            device_id={"fsdp": me + way * CORES},
+        )
+
+    def long_copy(at_long, way):
+        landing = from_low if way > 0 else from_high
+        side = 0 if way > 0 else 1
+        return pltpu.make_async_remote_copy(
+            src_ref=line.at[at_long],
+            dst_ref=landing.at[at_long],
+            send_sem=long_send.at[side, at_long],
+            recv_sem=long_recv.at[side, at_long],
+            device_id={"fsdp": me + way * CORES * across_size},
+        )
+
+    for steps in order:
+        at_long, at_across = spot(*steps)
+        pair = at_long * across_size + at_across
+        for copy in core_copies(at_long, at_across):
+            copy.wait_recv()
+        block = pair * CORES + core
+        start = pl.ds(pl.multiple_of(block * rows, rows), rows)
+        part[pair, :, :width] = (qkv_ref[start, :].astype(wide) + from_qkv[pair].astype(wide)).astype(low)
+        part[pair, :, width : width + square] = (
+            proj_ref[start, :].astype(wide) + from_proj[pair].astype(wide)
+        ).astype(low)
+        part[pair, :, width + square :] = (
+            small_ref[block].astype(wide) + from_small[pair].astype(wide)
+        ).astype(low)
+
+        if steps[1] < across_size - 1:
+            for way in (1, -1):
+                @pl.when((at_across - across) * way > 0)
+                def _():
+                    @pl.when(inside(across - way, across_size))
+                    def _():
+                        across_copy(at_long, at_across, way).wait_recv()
+                        landing = from_left if way > 0 else from_right
+                        part[pair] = (part[pair].astype(wide) + landing[pair].astype(wide)).astype(low)
+
+                    across_copy(at_long, at_across, way).start()
+
+    for step_long in range(long_size):
+        at_long = lax.rem(along + 1 + step_long, long_size)
+        pair = at_long * across_size + across
+        line[at_long] = part[pair]
+        for way in (1, -1):
+            @pl.when(inside(across - way, across_size))
+            def _():
+                across_copy(at_long, across, way).wait_recv()
+                landing = from_left if way > 0 else from_right
+                line[at_long] = (line[at_long].astype(wide) + landing[pair].astype(wide)).astype(low)
+
+        for way in (1, -1):
+            @pl.when(inside(along - way, long_size))
+            def _():
+                @pl.when((at_long - along) * way >= 0)
+                def _():
+                    long_copy(at_long, way).wait_recv()
+                    landing = from_low if way > 0 else from_high
+                    line[at_long] = (line[at_long].astype(wide) + landing[at_long].astype(wide)).astype(low)
+
+            @pl.when((at_long - along) * way > 0)
+            def _():
+                long_copy(at_long, way).start()
+
+    mine_ref[...] = line[along]
+    twin = lax.axis_index("dp")
+
+    def twin_copy(step):
+        return pltpu.make_async_remote_copy(
+            src_ref=mine_ref,
+            dst_ref=twins.at[step],
+            send_sem=twin_send.at[step],
+            recv_sem=twin_recv.at[step],
+            device_id={"dp": lax.rem(twin + step, replicas)},
+        )
+
+    for step in range(1, replicas):
+        twin_copy(step).start()
+    for step in range(1, replicas):
+        twin_copy(step).wait()
+    twins[0] = mine_ref[...]
+    total = jnp.zeros(mine_ref.shape, wide)
+    for rank in range(replicas):
+        total = total + twins[lax.rem(twin - rank + replicas, replicas)].astype(wide)
+    total = total * factor
+    qkv_out[...] = total[:, :width]
+    proj_out[...] = total[:, width : width + square]
+    small_out[...] = total[:, width + square :]
+
+    for steps in order:
+        at_long, at_across = spot(*steps)
+        for copy in core_copies(at_long, at_across):
+            copy.wait_send()
+        if steps[1] < across_size - 1:
+            for way in (1, -1):
+                @pl.when((at_across - across) * way > 0)
+                def _():
+                    across_copy(at_long, at_across, way).wait_send()
+
+    for step_long in range(long_size):
+        at_long = lax.rem(along + 1 + step_long, long_size)
+        for way in (1, -1):
+            @pl.when((at_long - along) * way > 0)
+            def _():
+                long_copy(at_long, way).wait_send()
+
+
+def scatter_all(owners, replicas, factor, qkv_term, proj_term, small):
+    long_size, across_size = grid_of(owners)
+    pairs = owners // CORES
+    rows = qkv_term.shape[0] // owners
+    width = qkv_term.shape[1]
+    square = proj_term.shape[1]
+    packed = width + square + LANES
+    low = jnp.bfloat16
+    block = (rows, packed)
+    dma = pltpu.SemaphoreType.DMA
+    return pl.pallas_call(
+        functools.partial(scatter_kernel, owners, replicas, factor),
+        name="scatter_all",
+        out_shape=(
+            jax.ShapeDtypeStruct((rows, width), jnp.float32),
+            jax.ShapeDtypeStruct((rows, square), jnp.float32),
+            jax.ShapeDtypeStruct((rows, LANES), jnp.float32),
+        ),
+        in_specs=[pl.BlockSpec(memory_space=pltpu.VMEM)] * 3,
+        out_specs=(pl.BlockSpec(memory_space=pltpu.VMEM),) * 3,
+        scratch_shapes=[
+            pltpu.VMEM((pairs, rows, width), low),
+            pltpu.VMEM((pairs, rows, square), low),
+            pltpu.VMEM((pairs, rows, LANES), low),
+            pltpu.VMEM((pairs,) + block, low),
+            pltpu.VMEM((pairs,) + block, low),
+            pltpu.VMEM((pairs,) + block, low),
+            pltpu.VMEM((long_size,) + block, low),
+            pltpu.VMEM((long_size,) + block, low),
+            pltpu.VMEM((long_size,) + block, low),
+            pltpu.VMEM(block, low),
+            pltpu.VMEM((replicas,) + block, low),
+            dma((3, pairs)),
+            dma((3, pairs)),
+            dma((2, pairs)),
+            dma((2, pairs)),
+            dma((2, long_size)),
+            dma((2, long_size)),
+            dma((replicas,)),
+            dma((replicas,)),
+        ],
+        compiler_params=pltpu.CompilerParams(
+            collective_id=1, has_side_effects=True, vmem_limit_bytes=60 * 2**20
+        ),
+    )(qkv_term, proj_term, small)
+
+
 def per_device(
     tokens, cotangent, patch_count, image_starts, qkv_weight, proj_weight, norm_gain, norm_shift
 ):
-    whole_qkv, whole_proj, whole_gain, whole_shift = (
-        lax.all_gather(qkv_weight, "fsdp", axis=0, tiled=True),
-        lax.all_gather(proj_weight, "fsdp", axis=0, tiled=True),
-        lax.all_gather(norm_gain, "fsdp", axis=0, tiled=True),
-        lax.all_gather(norm_shift, "fsdp", axis=0, tiled=True),
-    )
+    replicas = lax.axis_size("dp")
+    owners = lax.axis_size("fsdp")
+    rows, width = qkv_weight.shape
+    square = proj_weight.shape[1]
+    model = owners * rows
+    own_small = jnp.stack([norm_gain, norm_shift], axis=1)
+    own_small = jnp.pad(own_small, ((0, 0), (0, LANES - 2)))
+    own = jnp.concatenate([qkv_weight, proj_weight, own_small], axis=1)
+    whole_qkv, whole_proj, whole_small = gather_all(owners, own, width, square)
+    whole_small = whole_small[:, :, :2].reshape(model, 2)
     grad_block, qkv_term, proj_term, gain_term, shift_term = block_backward(
         tokens,
         cotangent,
@@ -93,40 +485,21 @@
         image_starts[0],
         whole_qkv,
         whole_proj,
-        whole_gain,
-        whole_shift,
-    )
-    replicas = lax.axis_size("dp")
-    owners = lax.axis_size("fsdp")
+        whole_small[:, 0],
+        whole_small[:, 1],
+    )
     factor = 1.0 / math.sqrt(tokens.shape[0] * replicas * owners)
-    terms = (qkv_term, proj_term, gain_term, shift_term)
-    summed = (
-        lax.psum_scatter(
-            terms[0].astype(jnp.bfloat16), "fsdp", scatter_dimension=0, tiled=True
-        ).astype(jnp.float32),
-        lax.psum_scatter(
-            terms[1].astype(jnp.bfloat16), "fsdp", scatter_dimension=0, tiled=True
-        ).astype(jnp.float32),
-        lax.psum_scatter(
-            terms[2].astype(jnp.bfloat16), "fsdp", scatter_dimension=0, tiled=True
-        ).astype(jnp.float32),
-        lax.psum_scatter(
-            terms[3].astype(jnp.bfloat16), "fsdp", scatter_dimension=0, tiled=True
-        ).astype(jnp.float32),
-    )
-    summed = (
-        lax.psum(summed[0].astype(jnp.bfloat16), "dp").astype(jnp.float32),
-        lax.psum(summed[1].astype(jnp.bfloat16), "dp").astype(jnp.float32),
-        lax.psum(summed[2].astype(jnp.bfloat16), "dp").astype(jnp.float32),
-        lax.psum(summed[3].astype(jnp.bfloat16), "dp").astype(jnp.float32),
-    )
-    return (
-        grad_block,
-        summed[0] * factor,
-        summed[1] * factor,
-        summed[2] * factor,
-        summed[3] * factor,
-    )
+    small = jnp.stack([gain_term, shift_term], axis=1).astype(jnp.bfloat16)
+    small = jnp.pad(small, ((0, 0), (0, LANES - 2))).reshape(owners, rows, LANES)
+    qkv_grad, proj_grad, small_grad = scatter_all(
+        owners,
+        replicas,
+        factor,
+        qkv_term.astype(jnp.bfloat16),
+        proj_term.astype(jnp.bfloat16),
+        small,
+    )
+    return (grad_block, qkv_grad, proj_grad, small_grad[:, 0], small_grad[:, 1])
 
 
 def solution(mesh):

time: 310 us -> 265 us (0.85)
  Pallas kernels: 0 us -> 163 us
  waiting for transfers between devices: 124 us -> 0 us
  blocking collectives: 71.8 us -> 0 us
  between operations: 15.8 us -> 1.44 us
  local copies, waits for them, and re-layouts: 8.52 us -> 12.2 us
  other arithmetic: 11.3 us -> 7.7 us
    pallas_call x0 -> x2, Pallas kernels: none -> 163 us  [the longest x1 104 us: scatter_all(): pl.pallas_call(functools.partial(scatter_kernel, owners, replicas, factor...]
    unnamed x2 -> x0, blocking collectives: 66.9 us -> none
    reduce_scatter x2 -> x0, waiting for transfers between devices: 55.1 us -> none  [the longest x1 55.1 us: per_device(): lax.psum_scatter(terms[0].astype(jnp.bfloat16), 'fsdp', scatter_dimension...]
    all_gather x2 -> x0, waiting for transfers between devices: 40.9 us -> none  [the longest x1 22.1 us: per_device(): lax.all_gather(qkv_weight, 'fsdp', axis=0, tiled=True)]
    psum x1 -> x0, waiting for transfers between devices: 26.2 us -> none  [per_device(): lax.psum(summed[0].astype(jnp.bfloat16), 'dp').astype(jnp.float32)]
    psum x1 -> x0, blocking collectives: 4.91 us -> none  [per_device(): lax.psum(summed[2].astype(jnp.bfloat16), 'dp').astype(jnp.float32)]
    mul x3 -> x0, other arithmetic: 4.09 us -> none  [the longest x1 1.94 us: per_device(): summed[0] * factor]
  transfers between devices with their start and end apart: 5 -> 0, of which waited for: 4 -> 0; matrix products, arithmetic and copies ran while one was open for 30% -> 0% of each run, Pallas kernels for 0% -> 0%
where the time goes in v1:
time: 265 us; the launch traced here: 264 us
  Pallas kernels  163 us (62%)
  matrix products  79 us (30%)
  local copies, waits for them, and re-layouts  12.2 us (5%)
  other arithmetic  7.7 us (3%)
    pallas_call x1, Pallas kernels, scatter_all(): pl.pallas_call(functools.partial(scatter_kernel, owners, replicas, factor...  104 us
    pallas_call x1, Pallas kernels, gather_all(): pl.pallas_call(functools.partial(gather_kernel, owners), name='gather_all...  59.6 us
    dot_general x1, matrix products, block_backward(): jnp.einsum('hqk,khe->qhe', grad_scores, keys, preferred_element_type=jnp....  15.6 us
    dot_general x1, matrix products, block_backward(): jnp.einsum('hqk,qhe->khe', grad_scores, queries, preferred_element_type=j...  14.4 us
    dot_general x1, matrix products, block_backward(): jnp.dot(grad_qkv, qkv_weight.T, preferred_element_type=jnp.float32)  7.96 us
    dot_general x1, matrix products, block_backward(): jnp.dot(hidden, qkv_weight, preferred_element_type=jnp.float32)  6.85 us
    dot_general x1, matrix products, block_backward(): jnp.einsum('qhe,khe->hqk', grad_heads, values, preferred_element_type=jnp...  6.61 us
    dot_general x1, matrix products, block_backward(): qkv_term = jnp.dot(hidden.T, grad_qkv, preferred_element_type=jnp.float32)  5.87 us

profile of v1, /device:TPU:0, one launch (start us, length us, event | category | flops | bytes accessed | tf_op | source)
XLA Modules:
  0.0 263.6 jit_solution(12408958993936281760)
XLA Ops:
  0.6 1.3 convert_reduce_fusion
  2.0 0.0 copy-start
  2.0 1.6 fusion.33
  3.5 0.7 pad_maximum_fusion.2
  4.2 0.1 copy.45
  4.3 1.1 fusion.60.own_ref
  5.4 59.6 %gather_all.1 = (bf16[1024,3072]{1,0:T(8,128)(2,1)}, bf16[1024,1024]{1,0:T(8,128)(2,1)S(1)}, bf16[16,64,128]{2,1,0:T(8,128)(2,1)S(1)}) custom-call(bf16[64,4224]{1,0:T(8,128)(2,1)S(1)} %fusion.60.own_ref), custom_call_target="tpu_custom_call" | custom-call | tf_op jit(solution)/shard_map/gather_all/pallas_call | solution.py:227
  65.0 0.9 slice_convert_fusion.1
  65.9 1.2 copy.62
  67.1 0.2 copy.63
  67.3 0.0 copy-done
  67.3 6.9 %convolution_convert_fusion.1 = bf16[384,3072]{1,0:T(8,128)(2,1)} fusion(bf16[1024,3072]{1,0:T(8,128)(2,1)} %get-tuple-element.12, bf16[384,1024]{1,0:T(8,128)(2,1)S(1)} %copy-done, f32[1024]{0:T(1024)S(1)} %bitcast.79, f32[1024]{0:T(1024)S(1)} %bitcast.75, f32[384]{0:T(512)S(1)} %add_rsqrt_fusion, f32[384]{0:T(512)S(1)} %broadcast_multiply_fusion.2), kind=kOutput, calls=%fused_computation.15 | convolution fusion | flops 2419458048 | bytes 9448448 | tf_op jit(solution)/shard_map/dot_general | solution.py:37
  74.2 4.3 %copy.48 = bf16[384,3072]{0,1:T(8,128)(2,1)} copy(bf16[384,3072]{1,0:T(8,128)(2,1)} %convolution_convert_fusion.1) | data formatting | bytes 4718592 | tf_op jit(solution)/shard_map/convert_element_type | solution.py:37
  79.1 3.0 %convolution_convert_fusion.3 = bf16[384,1024]{1,0:T(8,128)(2,1)} fusion(bf16[1024,1024]{1,0:T(8,128)(2,1)S(1)} %get-tuple-element.13, bf16[384,1024]{1,0:T(8,128)(2,1)} %param.9, pred[384]{0:T(512)(128)(4,1)S(1)} %iota_compare_fusion.2), kind=kOutput, calls=%fused_computation.43 | convolution fusion | flops 806092800 | bytes 3670400 | tf_op jit(solution)/shard_map/dot_general | solution.py:55
  82.2 2.3 copy.49
  84.4 0.0 copy-start.11
  84.5 0.0 copy-start.1
  84.5 6.6 %fusion.58 = f32[16,384,384]{1,2,0:T(8,128)} fusion(bf16[384,16,64]{0,2,1:T(8,128)(2,1)} %bitcast.70, bf16[384,3,16,64]{0,3,2,1:T(8,128)(2,1)} %bitcast.65), kind=kOutput, calls=%fused_computation.55 | convolution fusion | flops 301989888 | bytes 11010048 | tf_op jit(solution)/shard_map/qhe,khe->hqk/dot_general | solution.py:59
  91.1 0.0 copy-done.11
  91.1 0.1 convert_reduce_fusion.1
  91.1 0.2 compare_and_fusion
  91.3 0.0 copy-done.1
  91.3 5.6 %fusion.71 = (f32[16,384]{1,0:T(8,128)S(1)}, f32[16,384,384]{1,2,0:T(8,128)}) fusion(pred[384,384]{0,1:T(8,128)(4,1)S(1)} %compare_and_fusion, bf16[384,3,16,64]{0,3,2,1:T(8,128)(2,1)S(1)} %bitcast.66), kind=kOutput, calls=%fused_computation.80 | convolution fusion | flops 311427456 | bytes 11182080 | tf_op jit(solution)/shard_map/sub | solution.py:45
  96.9 15.6 %fusion.49 = bf16[384,1,16,64]{0,3,2,1:T(8,128)(2,1)} fusion(f32[16,384,384]{1,2,0:T(8,128)} %fusion.58, bf16[384,3,16,64]{0,3,2,1:T(8,128)(2,1)S(1)} %bitcast.67, f32[16,384,384]{1,2,0:T(8,128)} %get-tuple-element.26, f32[16,384]{1,0:T(8,128)S(1)} %get-tuple-element.25), kind=kOutput, calls=%fused_computation.46 | convolution fusion | flops 318904704 | bytes 39370752 | tf_op jit(solution)/shard_map/hqk,khe->qhe/dot_general | solution.py:65
  112.5 14.4 %fusion.46 = bf16[384,1,16,64]{0,3,2,1:T(8,128)(2,1)} fusion(f32[16,384,384]{1,2,0:T(8,128)} %fusion.58, bf16[384,3,16,64]{0,3,2,1:T(8,128)(2,1)S(1)} %bitcast.68, f32[16,384,384]{1,2,0:T(8,128)} %get-tuple-element.26, f32[16,384]{1,0:T(8,128)S(1)} %get-tuple-element.25), kind=kOutput, calls=%fused_computation.45 | convolution fusion | flops 318904704 | bytes 39370752 | tf_op jit(solution)/shard_map/hqk,qhe->khe/dot_general | solution.py:68
  126.9 0.0 copy-start.5
  126.9 0.0 copy-start.6
  126.9 5.8 %fusion.52 = bf16[384,1,16,64]{0,3,2,1:T(8,128)(2,1)S(1)} fusion(bf16[384,16,64]{0,2,1:T(8,128)(2,1)} %bitcast.71, f32[16,384,384]{1,2,0:T(8,128)} %get-tuple-element.26, f32[16,384]{1,0:T(8,128)S(1)} %get-tuple-element.25), kind=kOutput, calls=%fused_computation.47 | convolution fusion | flops 307101696 | bytes 11034624 | tf_op jit(solution)/shard_map/hqk,qhe->khe/dot_general | solution.py:60
  132.8 0.0 copy-done.5
  132.8 0.0 copy-done.6
  132.8 0.3 pad_maximum_fusion
  133.1 0.0 copy-start.2
  133.1 8.0 %fusion.32 = (bf16[1024]{0:T(1024)(128)(2,1)S(1)}, f32[384]{0:T(512)S(1)}, f32[384]{0:T(512)S(1)}, bf16[1024]{0:T(1024)(128)(2,1)S(1)}, f32[384,1024]{1,0:T(8,128)}) fusion(bf16[384,1024]{1,0:T(8,128)(2,1)S(1)} %copy-done, f32[384]{0:T(512)S(1)} %add_rsqrt_fusion, f32[384]{0:T(512)S(1)} %broadcast_multiply_fusion.2, f32[1024]{0:T(1024)S(1)} %bitcast.76, ...), kind=kOutput, calls=%fused_computation.37 | convolution fusion | flops 2419848192 | bytes 11024384 | tf_op jit(solution)/shard_map/dot_general | solution.py:73
  141.1 0.0 copy-done.2
  141.1 0.2 copy.61
  141.3 0.8 pad.9.clone
  142.1 0.0 copy-start.8
  142.1 4.6 %fusion.37 = bf16[16,64,384]{2,1,0:T(8,128)(2,1)S(1)} fusion(bf16[384,3,16,64]{0,3,2,1:T(8,128)(2,1)S(1)} %bitcast.69, f32[16,384,384]{1,2,0:T(8,128)} %get-tuple-element.26, f32[16,384]{1,0:T(8,128)S(1)} %get-tuple-element.25), kind=kOutput, calls=%fused_computation.40 | convolution fusion | flops 307101696 | bytes 11034624 | tf_op jit(solution)/shard_map/hqk,khe->qhe/dot_general | solution.py:49
  146.7 0.0 copy-start.3
  146.7 0.0 copy-done.8
  146.7 2.7 %convolution_convert_fusion.2.proj_ref = bf16[1024,1024]{1,0:T(8,128)(2,1)} fusion(bf16[384,1024]{0,1:T(8,128)(2,1)S(1)} %bitcast.84, bf16[384,1024]{1,0:T(8,128)(2,1)S(1)} %copy-done.8, pred[384]{0:T(512)(128)(4,1)S(1)} %iota_compare_fusion.2), kind=kOutput, calls=%fused_computation.23 | convolution fusion | flops 806748160 | bytes 3670400 | tf_op jit(solution)/shard_map/dot_general | solution.py:54
  149.4 0.0 copy-done.3
  149.4 5.9 %convolution_convert_fusion.qkv_ref = bf16[1024,3072]{1,0:T(8,128)(2,1)} fusion(bf16[384,3072]{0,1:T(8,128)(2,1)S(1)} %bitcast.73, bf16[384,1024]{1,0:T(8,128)(2,1)S(1)} %copy-done, f32[1024]{0:T(1024)S(1)} %bitcast.80, f32[1024]{0:T(1024)S(1)} %bitcast.77, f32[384]{0:T(512)S(1)} %add_rsqrt_fusion, f32[384]{0:T(512)S(1)} %broadcast_multiply_fusion.2), kind=kOutput, calls=%fused_computation.8 | convolution fusion | flops 2421424128 | bytes 9448448 | tf_op jit(solution)/shard_map/dot_general | solution.py:72
  155.3 0.0 copy-start.4
  155.3 0.0 copy-start.9
  155.3 103.6 %scatter_all.1 = (f32[64,3072]{1,0:T(8,128)}, f32[64,1024]{1,0:T(8,128)}, f32[64,128]{1,0:T(8,128)}) custom-call(bf16[1024,3072]{1,0:T(8,128)(2,1)} %convolution_convert_fusion.qkv_ref, bf16[1024,1024]{1,0:T(8,128)(2,1)} %convolution_convert_fusion.2.proj_ref, bf16[16,64,128]{2,1,0:T(8,128)(2,1)} %bitcast.74), custom_call_target="tpu_custom_call" | custom-call | tf_op jit(solution)/shard_map/scatter_all/pallas_call | solution.py:431
  258.9 0.0 copy-start.7
  258.9 1.6 slice_reduce_fusion
  260.4 0.0 copy-done.4
  260.4 0.0 copy-done.9
  260.4 0.0 copy-start.10
  260.5 1.5 fusion.31
  262.0 0.0 copy-done.7
  262.0 0.9 copy.67
  262.9 0.0 copy-done.10
  262.9 0.7 copy.68
  (7 shorter events, 0.0 us)
Async XLA Ops:
  2.0 65.4 %copy-start = (bf16[384,1024]{1,0:T(8,128)(2,1)S(1)}, bf16[384,1024]{1,0:T(8,128)(2,1)}, u32[]{:S(2)}) copy-start(bf16[384,1024]{1,0:T(8,128)(2,1)} %param.8) | copy-start | bytes 2359300
  84.4 6.6 %copy-start.11 = (s32[1,8]{1,0:T(1,128)S(1)}, s32[1,8]{1,0:T(1,128)}, u32[]{:S(2)}) copy-start(s32[1,8]{1,0:T(1,128)} %param.11) | copy-start | bytes 100
  84.5 6.9 %copy-start.1 = (bf16[384,3072]{0,1:T(8,128)(2,1)S(1)}, bf16[384,3072]{0,1:T(8,128)(2,1)}, u32[]{:S(2)}) copy-start(bf16[384,3072]{0,1:T(8,128)(2,1)} %copy.48) | copy-start | bytes 7077892
  126.9 5.8 %copy-start.5 = (bf16[384,1,16,64]{0,3,2,1:T(8,128)(2,1)S(1)}, bf16[384,1,16,64]{0,3,2,1:T(8,128)(2,1)}, u32[]{:S(2)}) copy-start(bf16[384,1,16,64]{0,3,2,1:T(8,128)(2,1)} %fusion.49) | copy-start | bytes 2359300
  126.9 5.8 %copy-start.6 = (bf16[384,1,16,64]{0,3,2,1:T(8,128)(2,1)S(1)}, bf16[384,1,16,64]{0,3,2,1:T(8,128)(2,1)}, u32[]{:S(2)}) copy-start(bf16[384,1,16,64]{0,3,2,1:T(8,128)(2,1)} %fusion.46) | copy-start | bytes 2359300
  133.1 8.0 %copy-start.2 = (bf16[384,3,16,64]{0,3,2,1:T(8,128)(2,1)}, bf16[384,3,16,64]{0,3,2,1:T(8,128)(2,1)S(1)}, u32[]{:S(2)}) copy-start(bf16[384,3,16,64]{0,3,2,1:T(8,128)(2,1)S(1)} %pad_maximum_fusion) | copy-start | bytes 7077892
  142.1 4.6 %copy-start.8 = (bf16[384,1024]{1,0:T(8,128)(2,1)S(1)}, bf16[384,1024]{1,0:T(8,128)(2,1)}, u32[]{:S(2)}) copy-start(bf16[384,1024]{1,0:T(8,128)(2,1)} %param.9) | copy-start | bytes 2359300
  146.7 2.7 %copy-start.3 = (bf16[384,3,16,64]{0,3,2,1:T(8,128)(2,1)S(1)}, bf16[384,3,16,64]{0,3,2,1:T(8,128)(2,1)}, u32[]{:S(2)}) copy-start(bf16[384,3,16,64]{0,3,2,1:T(8,128)(2,1)} %copy-done.2) | copy-start | bytes 7077892
  155.3 105.2 %copy-start.4 = (f32[384,1024]{1,0:T(8,128)S(1)}, f32[384,1024]{1,0:T(8,128)}, u32[]{:S(2)}) copy-start(f32[384,1024]{1,0:T(8,128)} %get-tuple-element.27) | copy-start | bytes 4718596
  155.3 105.2 %copy-start.9 = (bf16[384,1024]{1,0:T(8,128)(2,1)S(1)}, bf16[384,1024]{1,0:T(8,128)(2,1)}, u32[]{:S(2)}) copy-start(bf16[384,1024]{1,0:T(8,128)(2,1)} %param.9) | copy-start | bytes 2359300
  258.9 3.1 %copy-start.7 = (f32[64,3072]{1,0:T(8,128)S(1)}, f32[64,3072]{1,0:T(8,128)}, u32[]{:S(2)}) copy-start(f32[64,3072]{1,0:T(8,128)} %get-tuple-element.36) | copy-start | bytes 2359300
  260.4 2.4 copy-start.10

commit v2 on v1

--- a/solution.py
+++ b/solution.py
@@ -17,15 +17,80 @@
 masked_score = -1e30
 
 
+def dot_rows(a, b):
+    return lax.dot_general(a, b, (((1,), (1,)), ((), ())), preferred_element_type=jnp.float32)
+
+
+def dot_cols(a, b):
+    return lax.dot_general(a, b, (((0,), (0,)), ((), ())), preferred_element_type=jnp.float32)
+
+
+def attention_kernel(by_row, by_col, q_ref, k_ref, v_ref, g_ref, attended_ref, grad_ref):
+    at = pl.program_id(0)
+    heads = q_ref.shape[1] // HEAD_DIM
+    rows, lanes = q_ref.shape
+    model = attended_ref.shape[1] * pl.num_programs(0)
+    factor = HEAD_DIM ** (-0.5)
+    allowed = (by_row[...] == by_col[...]) & (by_row[...] >= 0)
+    head_of = lax.broadcasted_iota(jnp.int32, (1, lanes), 1) // HEAD_DIM
+    q, k, v, g = q_ref[...], k_ref[...], v_ref[...], g_ref[...]
+    sums = [jnp.zeros((rows, lanes), jnp.float32)] * 4
+    for head in range(heads):
+        mask = (head_of == head).astype(jnp.float32).astype(jnp.bfloat16)
+        q_own, k_own, v_own, g_own = q * mask, k * mask, v * mask, g * mask
+        scores = jnp.where(allowed, dot_rows(q_own, k) * factor, masked_score)
+        expon = jnp.exp(scores - jnp.max(scores, axis=1, keepdims=True))
+        probs = expon * (1.0 / jnp.sum(expon, axis=1, keepdims=True))
+        probs_low = probs.astype(jnp.bfloat16)
+        grad_probs = dot_rows(g_own, v)
+        inner = jnp.sum(probs * grad_probs, axis=1, keepdims=True)
+        grad_scores = (probs * (grad_probs - inner) * factor).astype(jnp.bfloat16)
+        terms = (
+            jnp.dot(probs_low, v_own, preferred_element_type=jnp.float32),
+            jnp.dot(grad_scores, k_own, preferred_element_type=jnp.float32),
+            dot_cols(grad_scores, q_own),
+            dot_cols(probs_low, g_own),
+        )
+        sums = [a + b for a, b in zip(sums, terms)]
+    attended_ref[...] = sums[0].astype(jnp.bfloat16)
+    for kind in range(3):
+        start = pl.multiple_of(kind * model + at * lanes, lanes)
+        grad_ref[:, pl.ds(start, lanes)] = sums[kind + 1].astype(jnp.bfloat16)
+
+
+def attention(qkv, grad_attended, marks):
+    rows, model = grad_attended.shape
+    lanes = 2 * HEAD_DIM
+    steps = model // lanes
+    spec = lambda shift: pl.BlockSpec((rows, lanes), lambda i: (0, shift * steps + i))
+    return pl.pallas_call(
+        attention_kernel,
+        name="attention",
+        grid=(steps,),
+        out_shape=(
+            jax.ShapeDtypeStruct((rows, model), jnp.bfloat16),
+            jax.ShapeDtypeStruct((rows, 3 * model), jnp.bfloat16),
+        ),
+        in_specs=[
+            pl.BlockSpec((rows, 1), lambda i: (0, 0)),
+            pl.BlockSpec((1, rows), lambda i: (0, 0)),
+            spec(0),
+            spec(1),
+            spec(2),
+            spec(0),
+        ],
+        out_specs=(spec(0), pl.BlockSpec((rows, 3 * model), lambda i: (0, 0))),
+        compiler_params=pltpu.CompilerParams(vmem_limit_bytes=40 * 2**20),
+    )(marks[:, None], marks[None, :], qkv, qkv, qkv, grad_attended)
+
+
 def block_backward(
     block_tokens, block_cot, live_count, starts, qkv_weight, proj_weight, norm_gain, norm_shift
 ):
     rows = block_tokens.shape[0]
-    factor = HEAD_DIM ** (-0.5)
     position = jnp.arange(rows, dtype=jnp.int32)
     live = position < live_count
     segment = jnp.sum((starts[None, :] <= position[:, None]).astype(jnp.int32), axis=1)
-    allowed = live[:, None] & live[None, :] & (segment[:, None] == segment[None, :])
     source = block_tokens.astype(jnp.float32)
     center = jnp.mean(source, axis=1, keepdims=True)
     centered = source - center
@@ -35,40 +100,12 @@
     gain = norm_gain.astype(jnp.float32)
     hidden = (normed * gain + norm_shift.astype(jnp.float32)).astype(jnp.bfloat16)
     qkv = jnp.dot(hidden, qkv_weight, preferred_element_type=jnp.float32).astype(jnp.bfloat16)
-    split = qkv.reshape(rows, 3, HEADS, HEAD_DIM)
-    queries = split[:, 0]
-    keys = split[:, 1]
-    values = split[:, 2]
-    scores = jnp.einsum("qhe,khe->hqk", queries, keys, preferred_element_type=jnp.float32) * factor
-    scores = jnp.where(allowed[None], scores, masked_score)
-    row_max = jnp.max(scores, axis=2, keepdims=True)
-    expon = jnp.exp(scores - row_max)
-    probs = expon / jnp.sum(expon, axis=2, keepdims=True)
-    probs_low = probs.astype(jnp.bfloat16)
-    attended = (
-        jnp.einsum("hqk,khe->qhe", probs_low, values, preferred_element_type=jnp.float32)
-        .reshape(rows, D)
-        .astype(jnp.bfloat16)
-    )
     masked_cot = jnp.where(live[:, None], block_cot, jnp.zeros_like(block_cot))
-    proj_term = jnp.dot(attended.T, masked_cot, preferred_element_type=jnp.float32)
     grad_attended = jnp.dot(masked_cot, proj_weight.T, preferred_element_type=jnp.float32).astype(
         jnp.bfloat16
     )
-    grad_heads = grad_attended.reshape(rows, HEADS, HEAD_DIM)
-    grad_probs = jnp.einsum("qhe,khe->hqk", grad_heads, values, preferred_element_type=jnp.float32)
-    grad_values = jnp.einsum(
-        "hqk,qhe->khe", probs_low, grad_heads, preferred_element_type=jnp.float32
-    ).astype(jnp.bfloat16)
-    grad_scores = probs * (grad_probs - jnp.sum(probs * grad_probs, axis=2, keepdims=True)) * factor
-    grad_scores = grad_scores.astype(jnp.bfloat16)
-    grad_queries = jnp.einsum(
-        "hqk,khe->qhe", grad_scores, keys, preferred_element_type=jnp.float32
-    ).astype(jnp.bfloat16)
-    grad_keys = jnp.einsum(
-        "hqk,qhe->khe", grad_scores, queries, preferred_element_type=jnp.float32
-    ).astype(jnp.bfloat16)
-    grad_qkv = jnp.stack([grad_queries, grad_keys, grad_values], axis=1).reshape(rows, 3 * D)
+    attended, grad_qkv = attention(qkv, grad_attended, jnp.where(live, segment, -1))
+    proj_term = jnp.dot(attended.T, masked_cot, preferred_element_type=jnp.float32)
     qkv_term = jnp.dot(hidden.T, grad_qkv, preferred_element_type=jnp.float32)
     grad_hidden = jnp.dot(grad_qkv, qkv_weight.T, preferred_element_type=jnp.float32)
     gain_term = jnp.sum(grad_hidden * normed, axis=0)
@@ -257,22 +294,21 @@
     rows = qkv_out.shape[0]
     width = qkv_out.shape[1]
     square = proj_out.shape[1]
-    pairs = owners // CORES
     wide = jnp.float32
     low = jnp.bfloat16
     greet(owners, replicas)
     sibling = {"fsdp": me + 1 - 2 * core}
 
-    order = [
-        (step_long, step_across)
-        for step_long in range(long_size)
-        for step_across in range(across_size)
-    ]
-
-    def spot(step_long, step_across):
-        at_long = lax.rem(along + 1 + step_long, long_size)
-        at_across = lax.rem(across + 1 + step_across, across_size)
-        return at_long, at_across
+    def outward(size):
+        return [sign * far for far in range(size - 1, 0, -1) for sign in (1, -1)] + [0]
+
+    order = [(up, out) for up in outward(long_size) for out in outward(across_size)]
+
+    def spot(up, out):
+        return along + up, across + out
+
+    def there(at_long, at_across):
+        return jnp.logical_and(inside(at_long, long_size), inside(at_across, across_size))
 
     def core_copies(at_long, at_across):
         pair = at_long * across_size + at_across
@@ -298,8 +334,10 @@
         return made
 
     for steps in order:
-        for copy in core_copies(*spot(*steps)):
-            copy.start()
+        @pl.when(there(*spot(*steps)))
+        def _():
+            for copy in core_copies(*spot(*steps)):
+                copy.start()
 
     def across_copy(at_long, at_across, way):
         pair = at_long * across_size + at_across
@@ -324,7 +362,7 @@
             device_id={"fsdp": me + way * CORES * across_size},
         )
 
-    for steps in order:
+    def join(steps):
         at_long, at_across = spot(*steps)
         pair = at_long * across_size + at_across
         for copy in core_copies(at_long, at_across):
@@ -338,21 +376,24 @@
         part[pair, :, width + square :] = (
             small_ref[block].astype(wide) + from_small[pair].astype(wide)
         ).astype(low)
-
-        if steps[1] < across_size - 1:
-            for way in (1, -1):
-                @pl.when((at_across - across) * way > 0)
-                def _():
-                    @pl.when(inside(across - way, across_size))
-                    def _():
-                        across_copy(at_long, at_across, way).wait_recv()
-                        landing = from_left if way > 0 else from_right
-                        part[pair] = (part[pair].astype(wide) + landing[pair].astype(wide)).astype(low)
-
-                    across_copy(at_long, at_across, way).start()
-
-    for step_long in range(long_size):
-        at_long = lax.rem(along + 1 + step_long, long_size)
+        if steps[1] != 0:
+            way = 1 if steps[1] > 0 else -1
+
+            @pl.when(inside(across - way, across_size))
+            def _():
+                across_copy(at_long, at_across, way).wait_recv()
+                landing = from_left if way > 0 else from_right
+                part[pair] = (part[pair].astype(wide) + landing[pair].astype(wide)).astype(low)
+
+            across_copy(at_long, at_across, way).start()
+
+    for steps in order:
+        @pl.when(there(*spot(*steps)))
+        def _():
+            join(steps)
+
+    def settle(up):
+        at_long = along + up
         pair = at_long * across_size + across
         line[at_long] = part[pair]
         for way in (1, -1):
@@ -363,17 +404,20 @@
                 line[at_long] = (line[at_long].astype(wide) + landing[pair].astype(wide)).astype(low)
 
         for way in (1, -1):
-            @pl.when(inside(along - way, long_size))
-            def _():
-                @pl.when((at_long - along) * way >= 0)
+            if up * way >= 0:
+                @pl.when(inside(along - way, long_size))
                 def _():
                     long_copy(at_long, way).wait_recv()
                     landing = from_low if way > 0 else from_high
                     line[at_long] = (line[at_long].astype(wide) + landing[at_long].astype(wide)).astype(low)
 
-            @pl.when((at_long - along) * way > 0)
-            def _():
+            if up * way > 0:
                 long_copy(at_long, way).start()
+
+    for up in outward(long_size):
+        @pl.when(inside(along + up, long_size))
+        def _():
+            settle(up)
 
     mine_ref[...] = line[along]
     twin = lax.axis_index("dp")
@@ -402,20 +446,19 @@
 
     for steps in order:
         at_long, at_across = spot(*steps)
-        for copy in core_copies(at_long, at_across):
-            copy.wait_send()
-        if steps[1] < across_size - 1:
-            for way in (1, -1):
-                @pl.when((at_across - across) * way > 0)
-                def _():
-                    across_copy(at_long, at_across, way).wait_send()
-
-    for step_long in range(long_size):
-        at_long = lax.rem(along + 1 + step_long, long_size)
-        for way in (1, -1):
-            @pl.when((at_long - along) * way > 0)
+
+        @pl.when(there(at_long, at_across))
+        def _():
+            for copy in core_copies(at_long, at_across):
+                copy.wait_send()
+            if steps[1] != 0:
+                across_copy(at_long, at_across, 1 if steps[1] > 0 else -1).wait_send()
+
+    for up in outward(long_size):
+        if up != 0:
+            @pl.when(inside(along + up, long_size))
             def _():
-                long_copy(at_long, way).wait_send()
+                long_copy(along + up, 1 if up > 0 else -1).wait_send()
 
 
 def scatter_all(owners, replicas, factor, qkv_term, proj_term, small):

time: 265 us -> 183 us (0.69)
  matrix products: 79 us -> 22.2 us
  Pallas kernels: 163 us -> 146 us
  local copies, waits for them, and re-layouts: 12.2 us -> 6.43 us
    dot_general x5 -> x0, matrix products: 47 us -> none  [the longest x1 15.6 us: block_backward(): jnp.einsum('hqk,khe->qhe', grad_scores, keys, preferred_element_type=jnp....]
    pallas_call x1, Pallas kernels: 104 us -> 71.4 us  [scatter_all(): pl.pallas_call(functools.partial(scatter_kernel, owners, replicas, factor...]
    pallas_call x0 -> x1, Pallas kernels: none -> 15 us  [attention(): pl.pallas_call(attention_kernel, name='attention', grid=(steps,), out_sha...]
    convert_element_type x2 -> x0, local copies, waits for them, and re-layouts: 6.56 us -> none  [the longest x1 4.28 us: block_backward(): jnp.dot(hidden, qkv_weight, preferred_element_type=jnp.float32)]
    sub x1 -> x0, matrix products: 5.57 us -> none  [block_backward(): expon = jnp.exp(scores - row_max)]
where the time goes in v2:
time: 183 us; the launch traced here: 182 us
  Pallas kernels  146 us (80%)
  matrix products  22.2 us (12%)
  local copies, waits for them, and re-layouts  6.43 us (4%)
  other arithmetic  6.17 us (3%)
    pallas_call x1, Pallas kernels, scatter_all(): pl.pallas_call(functools.partial(scatter_kernel, owners, replicas, factor...  71.4 us
    pallas_call x1, Pallas kernels, gather_all(): pl.pallas_call(functools.partial(gather_kernel, owners), name='gather_all...  59.6 us
    pallas_call x1, Pallas kernels, attention(): pl.pallas_call(attention_kernel, name='attention', grid=(steps,), out_sha...  15 us
    dot_general x1, matrix products, block_backward(): jnp.dot(hidden, qkv_weight, preferred_element_type=jnp.float32)  5.84 us
    dot_general x1, matrix products, block_backward(): jnp.dot(grad_qkv, qkv_weight.T, preferred_element_type=jnp.float32)  5.74 us
    dot_general x1, matrix products, block_backward(): qkv_term = jnp.dot(hidden.T, grad_qkv, preferred_element_type=jnp.float32)  5.69 us
    unnamed x25, local copies, waits for them, and re-layouts  4 us
    dot_general x1, matrix products, block_backward(): jnp.dot(attended.T, masked_cot, preferred_element_type=jnp.float32)  3.9 us

profile of v2, /device:TPU:0, one launch (start us, length us, event | category | flops | bytes accessed | tf_op | source)
XLA Modules:
  0.0 182.4 jit_solution(8219591099192578847)
XLA Ops:
  0.6 0.0 copy-start.9
  0.6 0.0 copy-start.7
  1.4 0.7 pad_maximum_fusion.1
  2.1 0.7 convert_reduce_fusion.1
  2.8 0.0 copy-start.5
  2.8 1.4 convert_reduce_fusion
  4.2 1.5 fusion.14
  5.7 0.1 copy.27
  5.8 0.1 reshape_select_fusion.by_row
  5.9 0.0 copy-done.9
  5.9 0.0 copy-done.7
  6.0 59.6 %gather_all.1 = (bf16[1024,3072]{1,0:T(8,128)(2,1)}, bf16[1024,1024]{1,0:T(8,128)(2,1)S(1)}, bf16[16,64,128]{2,1,0:T(8,128)(2,1)S(1)}) custom-call(bf16[64,4224]{1,0:T(8,128)(2,1)S(1)} %fusion.16.own_ref), custom_call_target="tpu_custom_call" | custom-call | tf_op jit(solution)/shard_map/gather_all/pallas_call | solution.py:264
  65.6 0.0 copy-done.5
  65.7 1.0 convolution_convert_fusion.3.g_ref
  66.7 0.0 copy-start.2
  66.7 0.1 slice_convert_fusion.1
  66.8 0.2 copy.34
  67.0 0.2 copy.35
  67.2 0.6 copy-done.2
  67.8 5.8 %convolution_convert_fusion.1.q_ref.k_ref.v_ref = bf16[384,3072]{1,0:T(8,128)(2,1)S(1)} fusion(bf16[1024,3072]{1,0:T(8,128)(2,1)} %get-tuple-element.14, bf16[384,1024]{1,0:T(8,128)(2,1)S(1)} %copy-done.2, f32[1024]{0:T(1024)S(1)} %bitcast.24, f32[1024]{0:T(1024)S(1)} %bitcast.20, f32[384]{0:T(512)S(1)} %add_rsqrt_fusion, f32[384]{0:T(512)S(1)} %broadcast_multiply_fusion.2), kind=kOutput, calls=%fused_computation.1 | convolution fusion | flops 2419458048 | bytes 9448448 | tf_op jit(solution)/shard_map/dot_general | solution.py:102
  73.7 0.0 copy-start.3
  73.7 15.0 %attention.1 = (bf16[384,1024]{1,0:T(8,128)(2,1)S(1)}, bf16[384,3072]{1,0:T(8,128)(2,1)S(1)}) custom-call(s32[384,1]{1,0:T(8,128)S(1)} %reshape_select_fusion.by_row, s32[1,384]{1,0:T(1,128)S(1)} %compare_select_fusion.by_col, bf16[384,3072]{1,0:T(8,128)(2,1)S(1)} %convolution_convert_fusion.1.q_ref.k_ref.v_ref, ...), custom_call_target="tpu_custom_call" | custom-call | tf_op jit(solution)/shard_map/attention/pallas_call | solution.py:66
  88.7 0.0 copy-start
  88.7 0.0 copy-done.3
  88.7 0.0 copy-start.6
  88.8 5.7 %fusion.13 = (bf16[1024]{0:T(1024)(128)(2,1)S(1)}, f32[384]{0:T(512)S(1)}, f32[384]{0:T(512)S(1)}, bf16[1024]{0:T(1024)(128)(2,1)S(1)}, f32[384,1024]{1,0:T(8,128)S(1)}) fusion(bf16[384,1024]{1,0:T(8,128)(2,1)S(1)} %copy-done.3, f32[384]{0:T(512)S(1)} %add_rsqrt_fusion, f32[384]{0:T(512)S(1)} %broadcast_multiply_fusion.2, f32[1024]{0:T(1024)S(1)} %bitcast.21, ...), kind=kOutput, calls=%fused_computation.18 | convolution fusion | flops 2419848192 | bytes 11024384 | tf_op jit(solution)/shard_map/dot_general | solution.py:110
  94.5 0.0 copy-done
  94.6 0.0 copy-done.6
  94.6 0.0 copy-start.1
  94.6 1.5 fusion.12
  96.1 0.2 copy.33
  96.3 0.8 pad.9.clone
  97.1 0.0 copy-done.1
  97.1 0.0 copy-start.4
  97.1 3.9 %convolution_convert_fusion.2.proj_ref = bf16[1024,1024]{1,0:T(8,128)(2,1)} fusion(bf16[384,1024]{1,0:T(8,128)(2,1)S(1)} %copy-done.1, bf16[384,1024]{1,0:T(8,128)(2,1)} %param.9, pred[384]{0:T(512)(128)(4,1)S(1)} %iota_compare_fusion.3), kind=kOutput, calls=%fused_computation.4 | convolution fusion | flops 806748160 | bytes 3670400 | tf_op jit(solution)/shard_map/dot_general | solution.py:108
  101.0 0.0 copy-done.4
  101.0 5.7 %convolution_convert_fusion.qkv_ref = bf16[1024,3072]{1,0:T(8,128)(2,1)} fusion(bf16[384,3072]{1,0:T(8,128)(2,1)S(1)} %get-tuple-element.16, bf16[384,1024]{1,0:T(8,128)(2,1)S(1)} %copy-done.4, f32[1024]{0:T(1024)S(1)} %bitcast.25, f32[1024]{0:T(1024)S(1)} %bitcast.23, f32[384]{0:T(512)S(1)} %add_rsqrt_fusion, f32[384]{0:T(512)S(1)} %broadcast_multiply_fusion.2), kind=kOutput, calls=%fused_computation | convolution fusion | flops 2421424128 | bytes 9448448 | tf_op jit(solution)/shard_map/dot_general | solution.py:109
  106.7 71.4 %scatter_all.1 = (f32[64,3072]{1,0:T(8,128)}, f32[64,1024]{1,0:T(8,128)}, f32[64,128]{1,0:T(8,128)}) custom-call(bf16[1024,3072]{1,0:T(8,128)(2,1)} %convolution_convert_fusion.qkv_ref, bf16[1024,1024]{1,0:T(8,128)(2,1)} %convolution_convert_fusion.2.proj_ref, bf16[16,64,128]{2,1,0:T(8,128)(2,1)} %bitcast.19), custom_call_target="tpu_custom_call" | custom-call | tf_op jit(solution)/shard_map/scatter_all/pallas_call | solution.py:474
  178.1 0.0 copy-start.8
  178.1 1.5 slice_reduce_fusion
  179.6 2.1 %copy.39 = f32[64,3072]{1,0:T(8,128)} copy(f32[64,3072]{1,0:T(8,128)} %get-tuple-element.38) | data formatting | bytes 1572864
  181.7 0.0 copy-done.8
  181.7 0.7 copy.40
  (9 shorter events, 0.1 us)
Async XLA Ops:
  0.6 5.3 %copy-start.9 = (bf16[64,1024]{1,0:T(8,128)(2,1)S(1)}, bf16[64,1024]{1,0:T(8,128)(2,1)}, u32[]{:S(2)}) copy-start(bf16[64,1024]{1,0:T(8,128)(2,1)} %param.13) | copy-start | bytes 393220
  0.6 5.3 %copy-start.7 = (bf16[64,3072]{1,0:T(8,128)(2,1)S(1)}, bf16[64,3072]{1,0:T(8,128)(2,1)}, u32[]{:S(2)}) copy-start(bf16[64,3072]{1,0:T(8,128)(2,1)} %param.12) | copy-start | bytes 1179652
  2.8 62.8 %copy-start.5 = (bf16[384,1024]{1,0:T(8,128)(2,1)S(1)}, bf16[384,1024]{1,0:T(8,128)(2,1)}, u32[]{:S(2)}) copy-start(bf16[384,1024]{1,0:T(8,128)(2,1)} %param.9) | copy-start | bytes 2359300
  66.7 1.1 copy-start.2
  73.7 15.1 %copy-start.3 = (bf16[384,1024]{1,0:T(8,128)(2,1)S(1)}, bf16[384,1024]{1,0:T(8,128)(2,1)}, u32[]{:S(2)}) copy-start(bf16[384,1024]{1,0:T(8,128)(2,1)} %param.8) | copy-start | bytes 2359300
  88.7 5.8 %copy-start = (bf16[384,1024]{1,0:T(8,128)(2,1)}, bf16[384,1024]{1,0:T(8,128)(2,1)S(1)}, u32[]{:S(2)}) copy-start(bf16[384,1024]{1,0:T(8,128)(2,1)S(1)} %get-tuple-element.17) | copy-start | bytes 2359300
  88.7 5.8 %copy-start.6 = (bf16[384,1024]{1,0:T(8,128)(2,1)S(1)}, bf16[384,1024]{1,0:T(8,128)(2,1)}, u32[]{:S(2)}) copy-start(bf16[384,1024]{1,0:T(8,128)(2,1)} %param.9) | copy-start | bytes 2359300
  94.6 2.5 %copy-start.1 = (bf16[384,1024]{1,0:T(8,128)(2,1)S(1)}, bf16[384,1024]{1,0:T(8,128)(2,1)}, u32[]{:S(2)}) copy-start(bf16[384,1024]{1,0:T(8,128)(2,1)} %copy-done) | copy-start | bytes 2359300
  97.1 3.9 %copy-start.4 = (bf16[384,1024]{1,0:T(8,128)(2,1)S(1)}, bf16[384,1024]{1,0:T(8,128)(2,1)}, u32[]{:S(2)}) copy-start(bf16[384,1024]{1,0:T(8,128)(2,1)} %param.8) | copy-start | bytes 2359300
  178.1 3.6 %copy-start.8 = (f32[64,1024]{1,0:T(8,128)S(1)}, f32[64,1024]{1,0:T(8,128)}, u32[]{:S(2)}) copy-start(f32[64,1024]{1,0:T(8,128)} %get-tuple-element.39) | copy-start | bytes 786436
